TPU v7x, 32 devices: a whole 2x2x4 slice. The times are simulated.
32 devices in a mesh: bump: 4 (over y, core), nx: 2 (over x), ny: 4 (over z).
Axes of the slice: x: 2, y: 2, z: 4, core: 2. Of those that a mesh axis runs over, the one named last changes fastest.
Arguments:
- payoff: float32 [262144], P(('nx', 'ny')), may hold values from -6 to 6
- positions: float32 [262144], P(('nx', 'ny')), may hold values from -20 to 20
- tables: float32 [8, 5, 262144], P('bump', None, ('nx', 'ny')), may hold values from 0.02 to 1, as said below
- offsets: int32 [8, 1024], P(None, ('nx', 'ny')), may hold values from -1 to 1
- vol_curve: float32 [8], replicated, may hold values from 0.5 to 1.2
- bucket: int32 [64], P('bump'), may hold values from 0 to 7
- bump_size: float32 [64], P('bump'), may hold values from 0.1 to 0.4
Outputs:
- bumped_values: float32 [64, 262144], P('bump', ('nx', 'ny'))
- vega: float32 [64], P('bump')
Inputs may be any that keep to these rules, and one draw needn't show every extreme that they name: `tables`: component 0 lies in [0.9, 1], components 1 and 3 in [0.1, 0.2], components 2 and 4 in [0.02, 0.06].
All inputs are finite; a program needn't handle non-finite values.
Results may differ from a plain program's by a relative error of at most 0.0003.
Values sent between devices are 32-bit elements; how exact they have to be, the bound alone decides.
A program may use at most 64 MiB of HBM per device.

v0:
```python
import jax
import jax.numpy as jnp
from jax import lax
from jax.sharding import PartitionSpec as P


def with_halo(array, sides, width):
    for axis, dim in sides:
        peers, length = (lax.axis_size(axis), array.shape[dim])
        up = [(i, (i + 1) % peers) for i in range(peers)]
        down = [(j, i) for i, j in up]
        last = lax.slice_in_dim(array, length - width, length, axis=dim)
        initial = lax.slice_in_dim(array, 0, width, axis=dim)
        before = lax.ppermute(last, axis, up)
        after = lax.ppermute(initial, axis, down)
        array = jnp.concatenate([before, array, after], axis=dim)
    return array


def advance(padded, table, branch_nodes, variance):
    count = padded.shape[-1] - 4

    def shifted(shift_by):
        return padded[..., 2 + shift_by : 2 + shift_by + count]

    upward = table[1] + variance * table[2]
    downward = table[3] + variance * table[4]
    middle = 1.0 - upward - downward
    low_case = upward * shifted(0) + middle * shifted(-1) + downward * shifted(-2)
    even_case = upward * shifted(1) + middle * shifted(0) + downward * shifted(-1)
    high_case = upward * shifted(2) + middle * shifted(1) + downward * shifted(0)
    mixed = jnp.where(
        branch_nodes == -1, low_case, jnp.where(branch_nodes == 0, even_case, high_case)
    )
    return table[0] * mixed


def on_device(payoff, positions, tables, offsets, vol_curve, bucket, bump_size):
    step_count = vol_curve.shape[0]
    node_count = payoff.shape[0]
    block_count = offsets.shape[1]
    block_len = node_count // block_count
    step_ids = jnp.arange(step_count, dtype=jnp.int32)
    sigma_bumps = vol_curve[None, :] + bump_size[:, None] * (
        bucket[:, None] == step_ids[None, :]
    ).astype(jnp.float32)
    sigma_rows = jnp.concatenate([vol_curve[None, :], sigma_bumps], axis=0)
    variance_rows = sigma_rows * sigma_rows
    values = jnp.broadcast_to(payoff[None, :], (sigma_rows.shape[0], node_count))
    all_tables = lax.all_gather(tables, "bump", axis=0, tiled=True)
    for step in reversed(range(step_count)):
        table = all_tables[step]
        padded = with_halo(values, ((("nx", "ny"), 1),), 2)
        branch_nodes = jnp.broadcast_to(offsets[step][:, None], (block_count, block_len)).reshape(
            node_count
        )
        values = advance(padded, table, branch_nodes[None, :], variance_rows[:, step : step + 1])
    base_values = values[0]
    bumped_values = values[1:]
    partial_sums = jnp.sum(positions[None, :] * (bumped_values - base_values[None, :]), axis=1)
    totals = lax.psum(partial_sums, ("nx", "ny"))
    return (bumped_values, totals / bump_size)


def solution(mesh):
    in_specs = (
        P(("nx", "ny")),
        P(("nx", "ny")),
        P("bump", None, ("nx", "ny")),
        P(None, ("nx", "ny")),
        P(),
        P("bump"),
        P("bump"),
    )
    out_specs = (P("bump", ("nx", "ny")), P("bump"))
    return jax.shard_map(
        on_device, mesh=mesh, in_specs=in_specs, out_specs=out_specs, check_vma=False
    )
```

profile of v0, /device:TPU:0, one launch (start us, length us, event | category | flops | bytes accessed | tf_op | source)
XLA Modules:
  0.0 239.4 jit_solution(8637577802408455618)
XLA Ops:
  7.3 3.5 %copy.10 = f32[2,5,32768]{2,1,0:T(8,128)} copy(f32[2,5,32768]{2,0,1:T(2,128)} %param.9) | data formatting | bytes 2621440 | tf_op args[2]
  10.8 6.0 %collective-permute-start.1 = (f32[17,2]{1,0:T(8,128)S(1)}, f32[17,2]{1,0:T(8,128)S(1)}, u32[]{:S(2)}, u32[]{:S(2)}) collective-permute-start(f32[17,2]{1,0:T(8,128)S(1)} %broadcast_in_dim.178), channel_id=1, source_target_pairs={{1,0},{2,1},{3,2},{4,3},{5,4},{6,5},{7,6},{0,7},{9,8},{10,9},{11,1... | collective-permute-start | bytes 416 | tf_op jit(solution)/shard_map/ppermute | solution.py:15
  18.4 0.6 eq.300
  19.8 0.6 eq.294
  22.0 0.6 eq.285
  24.4 47.5 %all-gather.2.cloned.1.call-done = f32[8,5,32768]{2,1,0:T(8,128)} async-done(((f32[2,5,32768]{2,1,0:T(8,128)}), f32[8,5,32768]{2,1,0:T(8,128)}) %all-gather.2.cloned.1.call-update) | async-done | bytes 5242896 | tf_op jit(solution)/shard_map/all_gather | solution.py:50
  71.9 10.1 %fusion.81 = (f32[1,1,32768]{2,1,0:T(1,128)S(1)}, f32[1,1,32768]{2,1,0:T(1,128)S(1)}, f32[1,1,32768]{2,1,0:T(1,128)}, f32[1,1,32768]{2,1,0:T(1,128)}, f32[1,1,32...) fusion(f32[8,5,32768]{2,1,0:T(8,128)} %all-gather.2.cloned.1.ca, ...), kind=kLoop, calls=%fused_computation.157 | loop fusion | bytes 4980736 | tf_op jit(solution)/shard_map/slice | solution.py:26
  82.0 10.3 %fusion.80 = (f32[1,1,32768]{2,1,0:T(1,128)S(1)}, f32[1,1,32768]{2,1,0:T(1,128)S(1)}, f32[1,1,32768]{2,1,0:T(1,128)}, f32[1,1,32768]{2,1,0:T(1,128)}, f32[1,1,32...) fusion(f32[8,5,32768]{2,1,0:T(8,128)} %all-gather.2.cloned.1.ca, ...), kind=kLoop, calls=%fused_computation.156 | loop fusion | bytes 4980736 | tf_op jit(solution)/shard_map/slice | solution.py:35
  92.5 5.4 %fusion.77 = f32[17,32768]{1,0:T(8,128)S(1)} fusion(f32[17,2]{1,0:T(8,128)S(1)} %collective-permute-done.1, f32[17,32768]{1,0:T(8,128)S(1)} %broadcast_in_dim.174, f32[17,2]{1,0:T(8,128)S(1)} %collective-permute-done, f32[32768]{0:T(1024)S(1)} %bitcast.124, f32[32768]{0:T(1024)S(1)} %bitcast.125, f32[32768]{0:T(1024)S(1)} %bitcast.126, ...), kind=kLoop, calls=%fused_computation.124 | loop fusion | flops 15597568 | bytes 5177684 | tf_op jit(solution)/shard_map/mul | solution.py:35
  98.0 1.6 copy-done.2
  99.7 1.5 collective-permute-start.2
  101.1 3.2 %collective-permute-start.3 = (f32[17,2]{1,0:T(8,128)S(1)}, f32[17,2]{1,0:T(8,128)S(1)}, u32[]{:S(2)}, u32[]{:S(2)}) collective-permute-start(f32[17,2]{1,0:T(8,128)S(1)} %get-tuple-element.57), channel_id=1, source_target_pairs={{1,0},{2,1},{3,2},{4,3},{5,4},{6,5},{7,6},{0,7},{9,8},{10,9},{11,1... | collective-permute-start | bytes 416 | tf_op jit(solution)/shard_map/ppermute | solution.py:15
  105.1 0.9 collective-permute-done.2
  106.6 10.1 %fusion.69 = f32[17,32768]{1,0:T(8,128)S(1)} fusion(f32[17,2]{1,0:T(8,128)} %copy-done.12, f32[17,32768]{1,0:T(8,128)} %copy-done.2, f32[17,2]{1,0:T(8,128)S(1)} %collective-permute-done.2, f32[32768]{0:T(1024)} %bitcast.121, f32[32768]{0:T(1024)} %bitcast.122, f32[32768]{0:T(1024)} %bitcast.118, f32[17]{0:T(128)} %get-tuple-element.78, ...), kind=kLoop, calls=%fused_computation.114 | loop fusion | flops 15597568 | bytes 5177684 | tf_op jit(solution)/shard_map/mul | solution.py:35
  116.8 0.7 fusion.88
  117.7 4.5 %collective-permute-start.5 = (f32[17,2]{1,0:T(8,128)S(1)}, f32[17,2]{1,0:T(8,128)}, u32[]{:S(2)}, u32[]{:S(2)}) collective-permute-start(f32[17,2]{1,0:T(8,128)S(1)} %get-tuple-element.55), channel_id=1, source_target_pairs={{1,0},{2,1},{3,2},{4,3},{5,4},{6,5},{7,6},{0,7},{9,8},{10,9},{11,1... | collective-permute-start | bytes 416 | tf_op jit(solution)/shard_map/ppermute | solution.py:15
  122.2 0.7 broadcast_in_dim.166
  122.9 1.4 eq.270
  124.3 6.4 %fusion.61 = f32[17,32768]{1,0:T(8,128)S(1)} fusion(f32[17,2]{1,0:T(8,128)} %collective-permute-done.5, f32[17,32768]{1,0:T(8,128)S(1)} %fusion.69, f32[17,2]{1,0:T(8,128)} %collective-permute-done.4, f32[32768]{0:T(1024)} %bitcast.116, f32[32768]{0:T(1024)} %bitcast.117, f32[32768]{0:T(1024)} %bitcast.113, f32[17]{0:T(128)} %get-tuple-element.79, ...), kind=kLoop, calls=%fused_computation.104 | loop fusion | flops 15597568 | bytes 5177684 | tf_op jit(solution)/shard_map/mul | solution.py:35
  130.7 1.6 copy-done
  132.4 0.8 collective-permute-start.6
  133.2 3.9 %collective-permute-start.7 = (f32[17,2]{1,0:T(8,128)S(1)}, f32[17,2]{1,0:T(8,128)S(1)}, u32[]{:S(2)}, u32[]{:S(2)}) collective-permute-start(f32[17,2]{1,0:T(8,128)S(1)} %get-tuple-element.53), channel_id=1, source_target_pairs={{1,0},{2,1},{3,2},{4,3},{5,4},{6,5},{7,6},{0,7},{9,8},{10,9},{11,1... | collective-permute-start | bytes 416 | tf_op jit(solution)/shard_map/ppermute | solution.py:15
  137.2 0.6 eq.267
  137.8 0.9 collective-permute-done.6
  139.4 10.2 %fusion.53 = f32[17,32768]{1,0:T(8,128)S(1)} fusion(f32[17,2]{1,0:T(8,128)} %copy-done.11, f32[17,32768]{1,0:T(8,128)} %copy-done, f32[17,2]{1,0:T(8,128)S(1)} %collective-permute-done.6, f32[32768]{0:T(1024)} %bitcast.111, f32[32768]{0:T(1024)} %bitcast.112, f32[32768]{0:T(1024)} %bitcast.108, f32[17]{0:T(128)} %get-tuple-element.80, f32[32768]{0:T(1024)} %bitcast.109, ...), kind=kLoop, calls=%fused_computation.94 | loop fusion | flops 15597568 | bytes 5177684 | tf_op jit(solution)/shard_map/mul | solution.py:35
  149.6 0.7 fusion.86
  150.3 0.8 collective-permute-start.8
  151.1 3.9 %collective-permute-start.9 = (f32[17,2]{1,0:T(8,128)S(1)}, f32[17,2]{1,0:T(8,128)}, u32[]{:S(2)}, u32[]{:S(2)}) collective-permute-start(f32[17,2]{1,0:T(8,128)S(1)} %get-tuple-element.51), channel_id=1, source_target_pairs={{1,0},{2,1},{3,2},{4,3},{5,4},{6,5},{7,6},{0,7},{9,8},{10,9},{11,1... | collective-permute-start | bytes 416 | tf_op jit(solution)/shard_map/ppermute | solution.py:15
  155.0 0.7 broadcast_in_dim.162
  155.7 1.4 eq.264
  157.1 6.4 %fusion.45 = f32[17,32768]{1,0:T(8,128)S(1)} fusion(f32[17,2]{1,0:T(8,128)} %collective-permute-done.9, f32[17,32768]{1,0:T(8,128)S(1)} %fusion.53, f32[17,2]{1,0:T(8,128)} %collective-permute-done.8, f32[32768]{0:T(1024)} %bitcast.106, f32[32768]{0:T(1024)} %bitcast.107, f32[32768]{0:T(1024)} %bitcast.103, f32[17]{0:T(128)} %get-tuple-element.81, ...), kind=kLoop, calls=%fused_computation.84 | loop fusion | flops 15597568 | bytes 5177684 | tf_op jit(solution)/shard_map/mul | solution.py:35
  163.6 1.6 copy-done.1
  165.2 0.8 collective-permute-start.10
  166.0 3.9 %collective-permute-start.11 = (f32[17,2]{1,0:T(8,128)S(1)}, f32[17,2]{1,0:T(8,128)S(1)}, u32[]{:S(2)}, u32[]{:S(2)}) collective-permute-start(f32[17,2]{1,0:T(8,128)S(1)} %get-tuple-element.49), channel_id=1, source_target_pairs={{1,0},{2,1},{3,2},{4,3},{5,4},{6,5},{7,6},{0,7},{9,8},{10,9},{11,1... | collective-permute-start | bytes 416 | tf_op jit(solution)/shard_map/ppermute | solution.py:15
  170.1 0.6 eq.261
  170.7 0.9 collective-permute-done.10
  171.7 10.1 %fusion.37 = f32[17,32768]{1,0:T(8,128)S(1)} fusion(f32[17,2]{1,0:T(8,128)S(1)} %collective-permute-done.11, f32[17,32768]{1,0:T(8,128)} %copy-done.1, f32[17,2]{1,0:T(8,128)S(1)} %collective-permute-done.10, f32[32768]{0:T(1024)} %bitcast.101, f32[32768]{0:T(1024)} %bitcast.102, f32[32768]{0:T(1024)} %bitcast.98, f32[17]{0:T(128)S(1)} %copy-done.17, ...), kind=kLoop, calls=%fused_computation.74 | loop fusion | flops 15597568 | bytes 5177684 | tf_op jit(solution)/shard_map/mul | solution.py:35
  181.9 0.8 collective-permute-start.12
  182.7 4.0 %collective-permute-start.13 = (f32[17,2]{1,0:T(8,128)S(1)}, f32[17,2]{1,0:T(8,128)S(1)}, u32[]{:S(2)}, u32[]{:S(2)}) collective-permute-start(f32[17,2]{1,0:T(8,128)S(1)} %get-tuple-element.47), channel_id=1, source_target_pairs={{1,0},{2,1},{3,2},{4,3},{5,4},{6,5},{7,6},{0,7},{9,8},{10,9},{11,1... | collective-permute-start | bytes 416 | tf_op jit(solution)/shard_map/ppermute | solution.py:15
  186.7 2.4 %fusion.82 = (f32[1,1,32768]{2,1,0:T(1,128)}, f32[1,1,32768]{2,1,0:T(1,128)S(1)}) fusion(f32[8,5,32768]{2,1,0:T(8,128)} %all-gather.2.cloned.1.call-done), kind=kLoop, calls=%fused_computation.158 | loop fusion | bytes 524288 | tf_op jit(solution)/shard_map/slice | solution.py:26
  189.2 5.4 %fusion.29 = f32[17,32768]{1,0:T(8,128)S(1)} fusion(f32[17,2]{1,0:T(8,128)S(1)} %collective-permute-done.13, f32[17,32768]{1,0:T(8,128)S(1)} %fusion.37, f32[17,2]{1,0:T(8,128)S(1)} %collective-permute-done.12, f32[32768]{0:T(1024)S(1)} %bitcast.96, f32[32768]{0:T(1024)S(1)} %bitcast.97, f32[32768]{0:T(1024)S(1)} %bitcast.94, f32[17]{0:T(128)S(1)} %copy-done.15, ...), kind=kLoop, calls=%fused_computation.64 | loop fusion | flops 15597568 | bytes 5177684 | tf_op jit(solution)/shard_map/mul | solution.py:35
  194.6 0.7 fusion.83
  195.6 4.4 %collective-permute-start.15 = (f32[17,2]{1,0:T(8,128)S(1)}, f32[17,2]{1,0:T(8,128)}, u32[]{:S(2)}, u32[]{:S(2)}) collective-permute-start(f32[17,2]{1,0:T(8,128)S(1)} %get-tuple-element.45), channel_id=1, source_target_pairs={{1,0},{2,1},{3,2},{4,3},{5,4},{6,5},{7,6},{0,7},{9,8},{10,9},{11,1... | collective-permute-start | bytes 416 | tf_op jit(solution)/shard_map/ppermute | solution.py:15
  200.0 0.7 broadcast_in_dim.191
  200.7 1.4 eq.303
  202.1 6.4 %fusion.21 = f32[17,32768]{1,0:T(8,128)S(1)} fusion(f32[17,2]{1,0:T(8,128)} %collective-permute-done.15, f32[17,32768]{1,0:T(8,128)S(1)} %fusion.29, f32[17,2]{1,0:T(8,128)} %collective-permute-done.14, f32[32768]{0:T(1024)S(1)} %bitcast.92, f32[32768]{0:T(1024)} %bitcast.93, f32[32768]{0:T(1024)} %bitcast.129, f32[17]{0:T(128)} %get-tuple-element.76, ...), kind=kLoop, calls=%fused_computation.54 | loop fusion | flops 15597568 | bytes 5177684 | tf_op jit(solution)/shard_map/mul | solution.py:35
  208.6 1.8 multiply_reduce_fusion
  210.4 21.6 %psum.7 = f32[16]{0:T(128)S(1)} all-reduce(f32[16]{0:T(128)S(1)} %get-tuple-element.2), channel_id=1, replica_groups=mesh['bump'=4,'nx'=2,'ny'=4] {'nx','ny'}, use_global_device_ids=true, to_apply=%region_1.2 | all-reduce | flops 16 | bytes 128 | tf_op jit(solution)/shard_map/psum | solution.py:61
  (99 shorter events, 9.5 us)
Async XLA Ops:
  7.2 3.6 %copy-start.7 = (f32[32768]{0:T(1024)S(1)}, f32[32768]{0:T(1024)}, u32[]{:S(2)}) copy-start(f32[32768]{0:T(1024)} %param.7) | copy-start | bytes 393220
  7.2 9.7 %copy-start.20 = (f32[8]{0:T(128)S(1)}, f32[8]{0:T(128)}, u32[]{:S(2)}) copy-start(f32[8]{0:T(128)} %param.11) | copy-start | bytes 100
  7.2 9.8 %copy-start.13 = (s32[8,128]{1,0:T(8,128)S(1)}, s32[8,128]{1,0:T(8,128)}, u32[]{:S(2)}) copy-start(s32[8,128]{1,0:T(8,128)} %param.10) | copy-start | bytes 12292
  7.2 16.4 %copy-start.22 = (f32[16]{0:T(128)S(1)}, f32[16]{0:T(128)}, u32[]{:S(2)}) copy-start(f32[16]{0:T(128)} %param.13) | copy-start | bytes 196
  7.2 16.4 %copy-start.21 = (s32[16]{0:T(128)S(1)}, s32[16]{0:T(128)}, u32[]{:S(2)}) copy-start(s32[16]{0:T(128)} %param.12) | copy-start | bytes 196
  7.2 64.7 %all-gather.2.cloned.1.call-start = ((), (), s32[]{:S(2)}) async-start(), calls=%async_computation | async-start | bytes 10485760 | tf_op jit(solution)/shard_map/all_gather | solution.py:50
  10.8 81.5 %collective-permute-start.1 = (f32[17,2]{1,0:T(8,128)S(1)}, f32[17,2]{1,0:T(8,128)S(1)}, u32[]{:S(2)}, u32[]{:S(2)}) collective-permute-start(f32[17,2]{1,0:T(8,128)S(1)} %broadcast_in_dim.178), channel_id=1, source_target_pairs={{1,0},{2,1},{3,2},{4,3},{5,4},{6,5},{7,6},{0,7},{9,8},{10,9},{11,1... | collective-permute-start | bytes 416 | tf_op jit(solution)/shard_map/ppermute | solution.py:15
  16.9 75.5 %collective-permute-start = (f32[17,2]{1,0:T(8,128)S(1)}, f32[17,2]{1,0:T(8,128)S(1)}, u32[]{:S(2)}, u32[]{:S(2)}) collective-permute-start(f32[17,2]{1,0:T(8,128)S(1)} %broadcast_in_dim.175), channel_id=1, source_target_pairs={{0,1},{1,2},{2,3},{3,4},{4,5},{5,6},{6,7},{7,0},{8,9},{9,10},{10,1... | collective-permute-start | bytes 416 | tf_op jit(solution)/shard_map/ppermute | solution.py:14
  98.0 1.6 copy-start.2
  99.7 6.4 %collective-permute-start.2 = (f32[17,2]{1,0:T(8,128)S(1)}, f32[17,2]{1,0:T(8,128)S(1)}, u32[]{:S(2)}, u32[]{:S(2)}) collective-permute-start(f32[17,2]{1,0:T(8,128)S(1)} %get-tuple-element.56), channel_id=1, source_target_pairs={{0,1},{1,2},{2,3},{3,4},{4,5},{5,6},{6,7},{7,0},{8,9},{9,10},{10,1... | collective-permute-start | bytes 416 | tf_op jit(solution)/shard_map/ppermute | solution.py:14
  101.1 4.9 %collective-permute-start.3 = (f32[17,2]{1,0:T(8,128)S(1)}, f32[17,2]{1,0:T(8,128)S(1)}, u32[]{:S(2)}, u32[]{:S(2)}) collective-permute-start(f32[17,2]{1,0:T(8,128)S(1)} %get-tuple-element.57), channel_id=1, source_target_pairs={{1,0},{2,1},{3,2},{4,3},{5,4},{6,5},{7,6},{0,7},{9,8},{10,9},{11,1... | collective-permute-start | bytes 416 | tf_op jit(solution)/shard_map/ppermute | solution.py:15
  106.0 0.6 copy-start.12
  106.6 15.5 %copy-start.19 = (pred[128]{0:T(512)(128)(4,1)S(1)}, pred[128]{0:T(512)(128)(4,1)}, u32[]{:S(2)}) copy-start(pred[128]{0:T(512)(128)(4,1)} %get-tuple-element.70) | copy-start | bytes 388
  117.4 6.8 %collective-permute-start.4 = (f32[17,2]{1,0:T(8,128)}, f32[17,2]{1,0:T(8,128)}, u32[]{:S(2)}, u32[]{:S(2)}) collective-permute-start(f32[17,2]{1,0:T(8,128)} %get-tuple-element.54), channel_id=1, source_target_pairs={{0,1},{1,2},{2,3},{3,4},{4,5},{5,6},{6,7},{7,0},{8,9},{9,10},{10,1... | collective-permute-start | bytes 416 | tf_op jit(solution)/shard_map/ppermute | solution.py:14
  117.7 6.5 %collective-permute-start.5 = (f32[17,2]{1,0:T(8,128)S(1)}, f32[17,2]{1,0:T(8,128)}, u32[]{:S(2)}, u32[]{:S(2)}) collective-permute-start(f32[17,2]{1,0:T(8,128)S(1)} %get-tuple-element.55), channel_id=1, source_target_pairs={{1,0},{2,1},{3,2},{4,3},{5,4},{6,5},{7,6},{0,7},{9,8},{10,9},{11,1... | collective-permute-start | bytes 416 | tf_op jit(solution)/shard_map/ppermute | solution.py:15
  124.3 12.9 %copy-start.18 = (pred[128]{0:T(512)(128)(4,1)S(1)}, pred[128]{0:T(512)(128)(4,1)}, u32[]{:S(2)}) copy-start(pred[128]{0:T(512)(128)(4,1)} %get-tuple-element.71) | copy-start | bytes 388
  130.7 1.6 copy-start
  132.4 6.4 %collective-permute-start.6 = (f32[17,2]{1,0:T(8,128)S(1)}, f32[17,2]{1,0:T(8,128)S(1)}, u32[]{:S(2)}, u32[]{:S(2)}) collective-permute-start(f32[17,2]{1,0:T(8,128)S(1)} %get-tuple-element.52), channel_id=1, source_target_pairs={{0,1},{1,2},{2,3},{3,4},{4,5},{5,6},{6,7},{7,0},{8,9},{9,10},{10,1... | collective-permute-start | bytes 416 | tf_op jit(solution)/shard_map/ppermute | solution.py:14
  133.2 5.6 %collective-permute-start.7 = (f32[17,2]{1,0:T(8,128)S(1)}, f32[17,2]{1,0:T(8,128)S(1)}, u32[]{:S(2)}, u32[]{:S(2)}) collective-permute-start(f32[17,2]{1,0:T(8,128)S(1)} %get-tuple-element.53), channel_id=1, source_target_pairs={{1,0},{2,1},{3,2},{4,3},{5,4},{6,5},{7,6},{0,7},{9,8},{10,9},{11,1... | collective-permute-start | bytes 416 | tf_op jit(solution)/shard_map/ppermute | solution.py:15
  138.8 0.6 copy-start.11
  139.4 15.6 %copy-start.16 = (pred[128]{0:T(512)(128)(4,1)S(1)}, pred[128]{0:T(512)(128)(4,1)}, u32[]{:S(2)}) copy-start(pred[128]{0:T(512)(128)(4,1)} %get-tuple-element.72) | copy-start | bytes 388
  150.3 6.8 %collective-permute-start.8 = (f32[17,2]{1,0:T(8,128)}, f32[17,2]{1,0:T(8,128)}, u32[]{:S(2)}, u32[]{:S(2)}) collective-permute-start(f32[17,2]{1,0:T(8,128)} %get-tuple-element.50), channel_id=1, source_target_pairs={{0,1},{1,2},{2,3},{3,4},{4,5},{5,6},{6,7},{7,0},{8,9},{9,10},{10,1... | collective-permute-start | bytes 416 | tf_op jit(solution)/shard_map/ppermute | solution.py:14
  151.1 6.0 %collective-permute-start.9 = (f32[17,2]{1,0:T(8,128)S(1)}, f32[17,2]{1,0:T(8,128)}, u32[]{:S(2)}, u32[]{:S(2)}) collective-permute-start(f32[17,2]{1,0:T(8,128)S(1)} %get-tuple-element.51), channel_id=1, source_target_pairs={{1,0},{2,1},{3,2},{4,3},{5,4},{6,5},{7,6},{0,7},{9,8},{10,9},{11,1... | collective-permute-start | bytes 416 | tf_op jit(solution)/shard_map/ppermute | solution.py:15
  157.1 12.9 %copy-start.14 = (pred[128]{0:T(512)(128)(4,1)S(1)}, pred[128]{0:T(512)(128)(4,1)}, u32[]{:S(2)}) copy-start(pred[128]{0:T(512)(128)(4,1)} %get-tuple-element.73) | copy-start | bytes 388
  157.1 14.6 %copy-start.17 = (f32[17]{0:T(128)S(1)}, f32[17]{0:T(128)}, u32[]{:S(2)}) copy-start(f32[17]{0:T(128)} %get-tuple-element.82) | copy-start | bytes 208
  163.5 1.6 copy-start.1
  165.2 6.4 %collective-permute-start.10 = (f32[17,2]{1,0:T(8,128)S(1)}, f32[17,2]{1,0:T(8,128)S(1)}, u32[]{:S(2)}, u32[]{:S(2)}) collective-permute-start(f32[17,2]{1,0:T(8,128)S(1)} %get-tuple-element.48), channel_id=1, source_target_pairs={{0,1},{1,2},{2,3},{3,4},{4,5},{5,6},{6,7},{7,0},{8,9},{9,10},{10,1... | collective-permute-start | bytes 416 | tf_op jit(solution)/shard_map/ppermute | solution.py:14
  166.0 5.6 %collective-permute-start.11 = (f32[17,2]{1,0:T(8,128)S(1)}, f32[17,2]{1,0:T(8,128)S(1)}, u32[]{:S(2)}, u32[]{:S(2)}) collective-permute-start(f32[17,2]{1,0:T(8,128)S(1)} %get-tuple-element.49), channel_id=1, source_target_pairs={{1,0},{2,1},{3,2},{4,3},{5,4},{6,5},{7,6},{0,7},{9,8},{10,9},{11,1... | collective-permute-start | bytes 416 | tf_op jit(solution)/shard_map/ppermute | solution.py:15
  171.6 17.5 %copy-start.3 = (f32[1,1,32768]{2,1,0:T(1,128)S(1)}, f32[1,1,32768]{2,1,0:T(1,128)}, u32[]{:S(2)}) copy-start(f32[1,1,32768]{2,1,0:T(1,128)} %get-tuple-element.40) | copy-start | bytes 393220
  171.6 17.5 %copy-start.4 = (f32[1,1,32768]{2,1,0:T(1,128)S(1)}, f32[1,1,32768]{2,1,0:T(1,128)}, u32[]{:S(2)}) copy-start(f32[1,1,32768]{2,1,0:T(1,128)} %get-tuple-element.41) | copy-start | bytes 393220
  171.7 17.5 %copy-start.5 = (f32[1,1,32768]{2,1,0:T(1,128)S(1)}, f32[1,1,32768]{2,1,0:T(1,128)}, u32[]{:S(2)}) copy-start(f32[1,1,32768]{2,1,0:T(1,128)} %get-tuple-element.7) | copy-start | bytes 393220
  171.7 17.5 %copy-start.6 = (f32[1,1,32768]{2,1,0:T(1,128)S(1)}, f32[1,1,32768]{2,1,0:T(1,128)}, u32[]{:S(2)}) copy-start(f32[1,1,32768]{2,1,0:T(1,128)} %get-tuple-element.8) | copy-start | bytes 393220
  171.7 17.5 %copy-start.8 = (pred[32768]{0:T(1024)(128)(4,1)S(1)}, pred[32768]{0:T(1024)(128)(4,1)}, u32[]{:S(2)}) copy-start(pred[32768]{0:T(1024)(128)(4,1)} %eq.300) | copy-start | bytes 98308
  171.7 17.5 %copy-start.9 = (pred[32768]{0:T(1024)(128)(4,1)S(1)}, pred[32768]{0:T(1024)(128)(4,1)}, u32[]{:S(2)}) copy-start(pred[32768]{0:T(1024)(128)(4,1)} %eq.261) | copy-start | bytes 98308
  171.7 17.5 %copy-start.15 = (f32[17]{0:T(128)S(1)}, f32[17]{0:T(128)}, u32[]{:S(2)}) copy-start(f32[17]{0:T(128)} %get-tuple-element.83) | copy-start | bytes 208
  181.9 7.2 %collective-permute-start.12 = (f32[17,2]{1,0:T(8,128)S(1)}, f32[17,2]{1,0:T(8,128)S(1)}, u32[]{:S(2)}, u32[]{:S(2)}) collective-permute-start(f32[17,2]{1,0:T(8,128)S(1)} %get-tuple-element.46), channel_id=1, source_target_pairs={{0,1},{1,2},{2,3},{3,4},{4,5},{5,6},{6,7},{7,0},{8,9},{9,10},{10,1... | collective-permute-start | bytes 416 | tf_op jit(solution)/shard_map/ppermute | solution.py:14
  182.7 6.4 %collective-permute-start.13 = (f32[17,2]{1,0:T(8,128)S(1)}, f32[17,2]{1,0:T(8,128)S(1)}, u32[]{:S(2)}, u32[]{:S(2)}) collective-permute-start(f32[17,2]{1,0:T(8,128)S(1)} %get-tuple-element.47), channel_id=1, source_target_pairs={{1,0},{2,1},{3,2},{4,3},{5,4},{6,5},{7,6},{0,7},{9,8},{10,9},{11,1... | collective-permute-start | bytes 416 | tf_op jit(solution)/shard_map/ppermute | solution.py:15
  195.3 6.8 %collective-permute-start.14 = (f32[17,2]{1,0:T(8,128)}, f32[17,2]{1,0:T(8,128)}, u32[]{:S(2)}, u32[]{:S(2)}) collective-permute-start(f32[17,2]{1,0:T(8,128)} %get-tuple-element.44), channel_id=1, source_target_pairs={{0,1},{1,2},{2,3},{3,4},{4,5},{5,6},{6,7},{7,0},{8,9},{9,10},{10,1... | collective-permute-start | bytes 416 | tf_op jit(solution)/shard_map/ppermute | solution.py:14
  195.6 6.5 %collective-permute-start.15 = (f32[17,2]{1,0:T(8,128)S(1)}, f32[17,2]{1,0:T(8,128)}, u32[]{:S(2)}, u32[]{:S(2)}) collective-permute-start(f32[17,2]{1,0:T(8,128)S(1)} %get-tuple-element.45), channel_id=1, source_target_pairs={{1,0},{2,1},{3,2},{4,3},{5,4},{6,5},{7,6},{0,7},{9,8},{10,9},{11,1... | collective-permute-start | bytes 416 | tf_op jit(solution)/shard_map/ppermute | solution.py:15
  202.1 6.5 %copy-start.10 = (f32[32768]{0:T(1024)S(1)}, f32[32768]{0:T(1024)}, u32[]{:S(2)}) copy-start(f32[32768]{0:T(1024)} %param.8) | copy-start | bytes 393220
  208.5 23.5 %copy-start.23 = (f32[16]{0:T(128)S(1)}, f32[16]{0:T(128)}, u32[]{:S(2)}) copy-start(f32[16]{0:T(128)} %param.13) | copy-start | bytes 196
Sparse Core Ops, SparseCore 0:
  10.9 60.9 all-gather.1
where the time goes:
time: 240 us; the launch traced here: 239 us
  other arithmetic  63.7 us (27%)
  waiting for transfers between devices  50.4 us (21%)
  local copies, waits for them, and re-layouts  50.1 us (21%)
  starting transfers between devices  39.2 us (16%)
  blocking collectives  21.6 us (9%)
  between operations  14.5 us (6%)
    mul x8, other arithmetic, advance(): return table[0] * mixed  60.6 us
    all_gather x1, waiting for transfers between devices, on_device(): all_tables = lax.all_gather(tables, 'bump', axis=0, tiled=True)  47.5 us
    ppermute x8, starting transfers between devices, with_halo(): after = lax.ppermute(initial, axis, down)  33.9 us
    psum x1, blocking collectives, on_device(): totals = lax.psum(partial_sums, ('nx', 'ny'))  21.6 us
    slice x2, local copies, waits for them, and re-layouts, advance(): upward = table[1] + variance * table[2]  12.5 us
    slice x1, local copies, waits for them, and re-layouts, advance(): return table[0] * mixed  10.3 us
    unnamed x49, local copies, waits for them, and re-layouts  9.57 us
    eq x8, local copies, waits for them, and re-layouts, advance(): branch_nodes == -1  5.98 us
  transfers between devices with their start and end apart: 17, of which 4 were waited for; matrix products, arithmetic and copies ran while one was open for 16% of the time, Pallas kernels for 0%

commit v1 on v0

v1 whole, which is shorter than its diff:
```python
import functools

import jax
import jax.numpy as jnp
from jax import lax
from jax.experimental import pallas as pl
from jax.experimental.pallas import tpu as pltpu
from jax.sharding import PartitionSpec as P

LANES = 128
SUB = 8
MESH = pl.DeviceIdType.MESH


def sweep_kernel(
    dims,
    vol_ref,
    payoff_ref,
    positions_ref,
    offsets_ref,
    tables_ref,
    rows_ref,
    sums_ref,
    tab,
    pay,
    offs,
    kmask,
    state,
    part,
    part2,
    tab_send,
    tab_recv,
    nb_send,
    nb_recv,
    own_sem,
    res_send,
    res_recv,
    ring_send,
    ring_recv,
    grp_send,
    grp_recv,
):
    n, nx, ny, steps, per, block_len = dims
    ring_size = nx * ny
    rows = payoff_ref.shape[0]
    quarter = rows // n
    ext = quarter + 2 * SUB
    me = lax.axis_index("bump")
    ring = lax.axis_index("nx") * ny + lax.axis_index("ny")

    def at(r, q):
        return {"bump": q, "nx": r // ny, "ny": r % ny}

    right = lax.rem(ring + 1, ring_size)
    left = lax.rem(ring + ring_size - 1, ring_size)
    mine = pl.ds(me * per, per)

    def piece(kind, q):
        if kind == 0:
            return q, ring, slice(q * quarter, (q + 1) * quarter), slice(SUB, SUB + quarter)
        if kind == 1:
            source = slice((q + 1) * quarter - 1, (q + 1) * quarter)
            target = (q + 1) % n
            return target, (right if q == n - 1 else ring), source, slice(SUB - 1, SUB)
        source = slice(q * quarter, q * quarter + 1)
        target = (q - 1) % n
        return target, (left if q == 0 else ring), source, slice(SUB + quarter, SUB + quarter + 1)

    def table_copy(kind, q):
        target, at_ring, source, landing = piece(kind, q)
        crosses = (kind == 1 and q == n - 1) or (kind == 2 and q == 0)
        src = tables_ref.at[:, source]
        dst = tab.at[mine, landing, 0:5]
        remote = pltpu.make_async_remote_copy(
            src_ref=src,
            dst_ref=dst,
            send_sem=tab_send.at[kind, q],
            recv_sem=tab_recv.at[kind, me],
            device_id=at(at_ring, target),
            device_id_type=MESH,
        )
        local = pltpu.make_async_copy(src, dst, tab_recv.at[kind, me])
        return target, crosses, remote, local

    for kind in (1, 2, 0):
        for q in range(n):
            target, crosses, remote, local = table_copy(kind, q)
            if crosses:
                remote.start()
            else:
                pl.when(me != target)(remote.start)
                pl.when(me == target)(local.start)

    def neighbour(i, src, dst, to):
        return pltpu.make_async_remote_copy(
            src_ref=src,
            dst_ref=dst,
            send_sem=nb_send.at[i],
            recv_sem=nb_recv.at[i],
            device_id=at(to, me),
            device_id_type=MESH,
        )

    near = [
        neighbour(0, payoff_ref.at[rows - SUB : rows], pay.at[0:SUB], right),
        neighbour(1, payoff_ref.at[0:SUB], pay.at[SUB + rows : SUB + rows + SUB], left),
        neighbour(2, offsets_ref, offs.at[0], right),
        neighbour(3, offsets_ref, offs.at[1], left),
    ]
    for copy in near:
        copy.start()
    own = pltpu.make_async_copy(payoff_ref, pay.at[SUB : SUB + rows], own_sem)
    own.start()
    for copy in near:
        copy.wait()
    own.wait()

    blocks = offsets_ref.shape[1]
    rows_per_block = block_len // LANES
    row_at = lax.broadcasted_iota(jnp.int32, (ext, blocks), 0) + me * quarter
    row_at = row_at + (rows - SUB)
    block_at = row_at // rows_per_block - blocks
    lane_at = lax.broadcasted_iota(jnp.int32, (ext, blocks), 1)
    for s in range(steps):
        def spread(line, shift):
            hit = lane_at == block_at + shift
            return jnp.where(hit, line.astype(jnp.float32), 0.0)

        picked = (
            spread(offsets_ref[s : s + 1, :], 0)
            + spread(offs[0, s : s + 1, :], blocks)
            + spread(offs[1, s : s + 1, :], -blocks)
        )
        branch = jnp.sum(picked, axis=1, keepdims=True)
        kmask[s] = jnp.broadcast_to(branch, (ext, LANES))

    state[0] = pay[pl.ds(pl.multiple_of(me * quarter, SUB), ext), :]
    lane = lax.broadcasted_iota(jnp.int32, (ext, LANES), 1)

    def waits(src):
        for kind in range(3):
            _, _, source, landing = piece(kind, 0)
            dst = tab.at[pl.ds(src * per, per), landing, 0:5]
            pltpu.make_async_copy(tables_ref.at[:, source], dst, tab_recv.at[kind, src]).wait()

    def shifts(x):
        f1 = pltpu.roll(x, LANES - 1, 1)
        f2 = pltpu.roll(x, LANES - 2, 1)
        b1 = pltpu.roll(x, 1, 1)
        b2 = pltpu.roll(x, 2, 1)
        f1 = jnp.where(lane >= LANES - 1, pltpu.roll(f1, ext - 1, 0), f1)
        f2 = jnp.where(lane >= LANES - 2, pltpu.roll(f2, ext - 1, 0), f2)
        b1 = jnp.where(lane < 1, pltpu.roll(b1, 1, 0), b1)
        b2 = jnp.where(lane < 2, pltpu.roll(b2, 1, 0), b2)
        return b2, b1, f1, f2

    for s in reversed(range(steps)):
        if s % per == per - 1:
            waits(s // per)
        w = vol_ref[s] * vol_ref[s]
        discount = tab[s, :, 0, :]
        slope_up = discount * tab[s, :, 2, :]
        slope_down = discount * tab[s, :, 4, :]
        up = discount * tab[s, :, 1, :] + w * slope_up
        down = discount * tab[s, :, 3, :] + w * slope_down
        middle = discount - up - down
        branch = kmask[s]
        low = branch < -0.5
        high = branch > 0.5

        def moved(x):
            b2, b1, f1, f2 = shifts(x)
            above = jnp.where(low, x, jnp.where(high, f2, f1))
            level = jnp.where(low, b1, jnp.where(high, f1, x))
            below = jnp.where(low, b2, jnp.where(high, x, b1))
            return above, level, below

        for g in [0] + list(range(s + 2, steps + 1)):
            above, level, below = moved(state[g])
            state[g] = up * above + middle * level + down * below
            if g == 0:
                state[s + 1] = slope_up * (above - level) + slope_down * (below - level)

    here = pl.ds(pl.multiple_of(me * quarter, SUB), quarter)
    for g in range(steps + 1):
        rows_ref[g, here, :] = state[g, SUB : SUB + quarter, :]
    weights = positions_ref[here, :]
    for s in range(steps):
        part[ring, s : s + 1, :] = jnp.sum(
            weights * state[s + 1, SUB : SUB + quarter, :], axis=0, keepdims=True
        )

    def result(m, d, slot):
        held = pl.ds(pl.multiple_of(jnp.bitwise_xor(me, m) * quarter, SUB), quarter)
        return pltpu.make_async_remote_copy(
            src_ref=rows_ref.at[:, held, :],
            dst_ref=rows_ref.at[:, held, :],
            send_sem=res_send.at[slot],
            recv_sem=res_recv.at[slot],
            device_id=at(ring, jnp.bitwise_xor(me, d)),
            device_id_type=MESH,
        )

    plan = []
    masks = [0]
    d = n // 2
    while d:
        plan += [(m, d) for m in masks]
        masks = masks + [m | d for m in masks]
        d //= 2
    slots = {m | d: i for i, (m, d) in enumerate(plan)}
    copies = [result(m, d, i) for i, (m, d) in enumerate(plan)]
    for i, (m, d) in enumerate(plan):
        if m == 0:
            copies[i].start()

    ring_copies = []
    for i in range(1, ring_size):
        to = lax.rem(ring + i, ring_size)
        ring_copies.append(
            pltpu.make_async_remote_copy(
                src_ref=part.at[ring],
                dst_ref=part.at[ring],
                send_sem=ring_send.at[i],
                recv_sem=ring_recv.at[i],
                device_id=at(to, me),
                device_id_type=MESH,
            )
        )
    for copy in ring_copies:
        copy.start()
    for i, copy in enumerate(ring_copies, 1):
        copy.wait_send()
        src = lax.rem(ring + ring_size - i, ring_size)
        pltpu.make_async_copy(part.at[src], part.at[src], ring_recv.at[i]).wait()
    part2[me] = jnp.sum(part[...], axis=0)
    grp_copies = []
    for i in range(1, n):
        grp_copies.append(
            pltpu.make_async_remote_copy(
                src_ref=part2.at[me],
                dst_ref=part2.at[me],
                send_sem=grp_send.at[i],
                recv_sem=grp_recv.at[i],
                device_id=at(ring, lax.rem(me + i, n)),
                device_id_type=MESH,
            )
        )
    for copy in grp_copies:
        copy.start()

    for i, (m, d) in enumerate(plan):
        if m != 0:
            copies[slots[m]].wait_recv()
            copies[i].start()
    for i, copy in enumerate(grp_copies, 1):
        copy.wait_send()
        src = lax.rem(me + n - i, n)
        pltpu.make_async_copy(part2.at[src], part2.at[src], grp_recv.at[i]).wait()
    sums_ref[...] = jnp.sum(part2[...], axis=0)
    forwarded = {m for m, _ in plan if m}
    for i, (m, d) in enumerate(plan):
        copies[i].wait_send()
        if m | d not in forwarded:
            copies[i].wait_recv()
    for kind in range(3):
        for q in range(n):
            target, crosses, remote, _ = table_copy(kind, q)
            if crosses:
                remote.wait_send()
            else:
                pl.when(me != target)(remote.wait_send)


def spread_kernel(vol_ref, bucket_ref, bump_ref, rows_ref, sums_ref, out_ref, vega_ref):
    curves = bucket_ref.shape[0]
    base = rows_ref[0]
    for b in range(curves):
        s = bucket_ref[b]
        change = bump_ref[b] * (2.0 * vol_ref[s] + bump_ref[b])
        out_ref[b // SUB, :, b % SUB, :] = base + change * rows_ref[s + 1]

    @pl.when(pl.program_id(0) == 0)
    def _():
        lane = lax.broadcasted_iota(jnp.int32, (1, curves), 1)
        total = jnp.zeros((1, curves), jnp.float32)
        for b in range(curves):
            s = bucket_ref[b]
            slope = 2.0 * vol_ref[s] + bump_ref[b]
            weighted = jnp.sum(sums_ref[pl.ds(s, 1), :], axis=1, keepdims=True)
            total = jnp.where(lane == b, slope * weighted, total)
        vega_ref[...] = total


def on_device(n, nx, ny, payoff, positions, tables, offsets, vol_curve, bucket, bump_size):
    steps = vol_curve.shape[0]
    per, comps, nodes = tables.shape
    curves = bucket.shape[0]
    rows = nodes // LANES
    block_len = nodes // offsets.shape[1]
    quarter = rows // n
    ext = quarter + 2 * SUB
    ring = nx * ny
    tiles = tables.reshape(per, comps, rows, LANES).transpose(0, 2, 1, 3)
    dma = pltpu.SemaphoreType.DMA
    vmem = pl.BlockSpec(memory_space=pltpu.VMEM)
    smem = pl.BlockSpec(memory_space=pltpu.SMEM)
    moved, sums = pl.pallas_call(
        functools.partial(sweep_kernel, (n, nx, ny, steps, per, block_len)),
        out_shape=(
            jax.ShapeDtypeStruct((steps + 1, rows, LANES), jnp.float32),
            jax.ShapeDtypeStruct((steps, LANES), jnp.float32),
        ),
        in_specs=[smem, vmem, vmem, vmem, pl.BlockSpec(memory_space=pl.ANY)],
        out_specs=(vmem, vmem),
        scratch_shapes=[
            pltpu.VMEM((steps, ext, SUB, LANES), jnp.float32),
            pltpu.VMEM((rows + 2 * SUB, LANES), jnp.float32),
            pltpu.VMEM((2,) + offsets.shape, jnp.int32),
            pltpu.VMEM((steps, ext, LANES), jnp.float32),
            pltpu.VMEM((steps + 1, ext, LANES), jnp.float32),
            pltpu.VMEM((ring, steps, LANES), jnp.float32),
            pltpu.VMEM((n, steps, LANES), jnp.float32),
            dma((3, n)),
            dma((3, n)),
            dma((4,)),
            dma((4,)),
            dma,
            dma((n - 1,)),
            dma((n - 1,)),
            dma((ring,)),
            dma((ring,)),
            dma((n,)),
            dma((n,)),
        ],
        compiler_params=pltpu.CompilerParams(has_side_effects=True),
        name="sweep",
    )(
        vol_curve,
        payoff.reshape(rows, LANES),
        positions.reshape(rows, LANES),
        offsets,
        tiles,
    )
    grid = n
    groups = curves // SUB
    bumped, vega = pl.pallas_call(
        spread_kernel,
        grid=(grid,),
        out_shape=(
            jax.ShapeDtypeStruct((groups, rows, SUB, LANES), jnp.float32),
            jax.ShapeDtypeStruct((1, curves), jnp.float32),
        ),
        in_specs=[
            smem,
            smem,
            smem,
            pl.BlockSpec((steps + 1, rows // grid, LANES), lambda i: (0, i, 0)),
            pl.BlockSpec((steps, LANES), lambda i: (0, 0)),
        ],
        out_specs=(
            pl.BlockSpec((groups, rows // grid, SUB, LANES), lambda i: (0, i, 0, 0)),
            pl.BlockSpec((1, curves), lambda i: (0, 0)),
        ),
        name="spread",
    )(vol_curve, bucket, bump_size, moved, sums)
    bumped = bumped.transpose(0, 2, 1, 3).reshape(curves, nodes)
    return bumped, vega.reshape(curves)


def solution(mesh):
    shape = dict(mesh.shape)
    in_specs = (
        P(("nx", "ny")),
        P(("nx", "ny")),
        P("bump", None, ("nx", "ny")),
        P(None, ("nx", "ny")),
        P(),
        P("bump"),
        P("bump"),
    )
    out_specs = (P("bump", ("nx", "ny")), P("bump"))
    body = functools.partial(on_device, shape["bump"], shape["nx"], shape["ny"])
    return jax.shard_map(body, mesh=mesh, in_specs=in_specs, out_specs=out_specs, check_vma=False)
```

time: 240 us -> 46 us (0.19)
  other arithmetic: 63.7 us -> 0 us
  waiting for transfers between devices: 50.4 us -> 0 us
  local copies, waits for them, and re-layouts: 50.1 us -> 4.5 us
  Pallas kernels: 0 us -> 40.6 us
  starting transfers between devices: 39.2 us -> 0 us
  blocking collectives: 21.6 us -> 0 us
  between operations: 14.5 us -> 0.65 us
    mul x9 -> x0, other arithmetic: 60.7 us -> none  [the longest x8 60.6 us: advance(): return table[0] * mixed]
    all_gather x1 -> x0, waiting for transfers between devices: 47.5 us -> none  [on_device(): all_tables = lax.all_gather(tables, 'bump', axis=0, tiled=True)]
    pallas_call x0 -> x2, Pallas kernels: none -> 40.6 us  [the longest x1 36.3 us: on_device(): pl.pallas_call(functools.partial(sweep_kernel, (n, nx, ny, steps, per, bl...]
    ppermute x16 -> x0, starting transfers between devices: 39.1 us -> none  [the longest x8 33.9 us: with_halo(): after = lax.ppermute(initial, axis, down)]
    slice x12 -> x0, local copies, waits for them, and re-layouts: 25.2 us -> none  [the longest x2 12.5 us: advance(): upward = table[1] + variance * table[2]]
    psum x1 -> x0, blocking collectives: 21.6 us -> none  [on_device(): totals = lax.psum(partial_sums, ('nx', 'ny'))]
    eq x16 -> x0, local copies, waits for them, and re-layouts: 11.2 us -> none  [the longest x8 5.98 us: advance(): branch_nodes == -1]
    unnamed x49 -> x0, local copies, waits for them, and re-layouts: 9.57 us -> none
  transfers between devices with their start and end apart: 17 -> 0, of which waited for: 4 -> 0; matrix products, arithmetic and copies ran while one was open for 16% -> 0% of each run, Pallas kernels for 0% -> 0%
where the time goes in v1:
time: 46 us; the launch traced here: 45.8 us
  Pallas kernels  40.6 us (88%)
  local copies, waits for them, and re-layouts  4.5 us (10%)
  between operations  0.65 us (1%)
    pallas_call x1, Pallas kernels, on_device(): pl.pallas_call(functools.partial(sweep_kernel, (n, nx, ny, steps, per, bl...  36.3 us
    reshape x2, local copies, waits for them, and re-layouts, on_device(): tiles = tables.reshape(per, comps, rows, LANES).transpose(0, 2, 1, 3)  4.5 us
    pallas_call x1, Pallas kernels, on_device(): pl.pallas_call(spread_kernel, grid=(grid,), out_shape=(jax.ShapeDtypeStru...  4.34 us

profile of v1, /device:TPU:0, one launch (start us, length us, event | category | flops | bytes accessed | tf_op | source)
XLA Modules:
  0.0 45.8 jit_solution(598274042638326564)
XLA Ops:
  0.6 2.4 %reshape.21 = f32[2,5,256,128]{3,2,0,1:T(8,128)S(1)} reshape(f32[2,5,32768]{2,0,1:T(2,128)} %param.9) | data formatting | bytes 2621440 | tf_op jit(solution)/shard_map/reshape | solution.py:304
  3.0 2.1 %copy.11 = f32[2,5,256,128]{3,1,2,0:T(8,128)} copy(f32[2,5,256,128]{3,2,0,1:T(8,128)S(1)} %reshape.21) | data formatting | bytes 2621440 | tf_op jit(solution)/shard_map/reshape | solution.py:304
  5.1 36.3 %sweep.1 = (f32[9,256,128]{2,1,0:T(8,128)}, f32[8,128]{1,0:T(8,128)}) custom-call(f32[8]{0:T(128)} %vol_ref.3, f32[256,128]{1,0:T(8,128)} %bitcast.12, f32[256,128]{1,0:T(8,128)} %bitcast.13, s32[8,128]{1,0:T(8,128)} %offsets_ref.1, f32[2,256,5,128]{3,2,1,0:T(8,128)} %bitcast.11), custom_call_target="tpu_custom_call" | custom-call | tf_op jit(solution)/shard_map/sweep/pallas_call | solution.py:308
  41.4 4.3 %spread.1 = (f32[2,256,8,128]{3,2,1,0:T(8,128)}, f32[1,16]{1,0:T(1,128)}) custom-call(f32[8]{0:T(128)} %vol_ref.3, s32[16]{0:T(128)} %bucket_ref.1, f32[16]{0:T(128)} %bump_ref.1, f32[9,256,128]{2,1,0:T(8,128)} %get-tuple-element.6.rows_ref, f32[8,128]{1,0:T(8,128)} %get-tuple-element.7.sums_ref), custom_call_target="tpu_custom_call" | custom-call | tf_op jit(solution)/shard_map/spread/pallas_call | solution.py:347

commit v2 on v1

--- a/solution.py
+++ b/solution.py
@@ -40,11 +40,13 @@
     grp_send,
     grp_recv,
 ):
-    n, nx, ny, steps, per, block_len = dims
+    n, nx, ny, steps, per, block_len, chunks = dims
     ring_size = nx * ny
     rows = payoff_ref.shape[0]
     quarter = rows // n
     ext = quarter + 2 * SUB
+    span = quarter // chunks
+    wide = span + 2 * SUB
     me = lax.axis_index("bump")
     ring = lax.axis_index("nx") * ny + lax.axis_index("ny")
 
@@ -53,43 +55,6 @@
 
     right = lax.rem(ring + 1, ring_size)
     left = lax.rem(ring + ring_size - 1, ring_size)
-    mine = pl.ds(me * per, per)
-
-    def piece(kind, q):
-        if kind == 0:
-            return q, ring, slice(q * quarter, (q + 1) * quarter), slice(SUB, SUB + quarter)
-        if kind == 1:
-            source = slice((q + 1) * quarter - 1, (q + 1) * quarter)
-            target = (q + 1) % n
-            return target, (right if q == n - 1 else ring), source, slice(SUB - 1, SUB)
-        source = slice(q * quarter, q * quarter + 1)
-        target = (q - 1) % n
-        return target, (left if q == 0 else ring), source, slice(SUB + quarter, SUB + quarter + 1)
-
-    def table_copy(kind, q):
-        target, at_ring, source, landing = piece(kind, q)
-        crosses = (kind == 1 and q == n - 1) or (kind == 2 and q == 0)
-        src = tables_ref.at[:, source]
-        dst = tab.at[mine, landing, 0:5]
-        remote = pltpu.make_async_remote_copy(
-            src_ref=src,
-            dst_ref=dst,
-            send_sem=tab_send.at[kind, q],
-            recv_sem=tab_recv.at[kind, me],
-            device_id=at(at_ring, target),
-            device_id_type=MESH,
-        )
-        local = pltpu.make_async_copy(src, dst, tab_recv.at[kind, me])
-        return target, crosses, remote, local
-
-    for kind in (1, 2, 0):
-        for q in range(n):
-            target, crosses, remote, local = table_copy(kind, q)
-            if crosses:
-                remote.start()
-            else:
-                pl.when(me != target)(remote.start)
-                pl.when(me == target)(local.start)
 
     def neighbour(i, src, dst, to):
         return pltpu.make_async_remote_copy(
@@ -109,6 +74,54 @@
     ]
     for copy in near:
         copy.start()
+
+    last = chunks + 1
+
+    def piece(kind, q):
+        if kind == 0:
+            source = slice((q + 1) * quarter - 1, (q + 1) * quarter)
+            target = (q + 1) % n
+            return target, (right if q == n - 1 else ring), source, slice(SUB - 1, SUB)
+        if kind == last:
+            source = slice(q * quarter, q * quarter + 1)
+            target = (q - 1) % n
+            landing = slice(SUB + quarter, SUB + quarter + 1)
+            return target, (left if q == 0 else ring), source, landing
+        lo = 0 if kind == 1 else (kind - 1) * span + SUB
+        hi = quarter if kind == chunks else kind * span + SUB
+        source = slice(q * quarter + lo, q * quarter + hi)
+        return q, ring, source, slice(SUB + lo, SUB + hi)
+
+    def table_copy(kind, q):
+        target, at_ring, source, landing = piece(kind, q)
+        crosses = (kind == 0 and q == n - 1) or (kind == last and q == 0)
+        src = tables_ref.at[:, source]
+        dst = tab.at[me, :, landing]
+
+        def remote():
+            return pltpu.make_async_remote_copy(
+                src_ref=src,
+                dst_ref=dst,
+                send_sem=tab_send.at[kind, q],
+                recv_sem=tab_recv.at[kind, me],
+                device_id=at(at_ring, target),
+                device_id_type=MESH,
+            )
+
+        def local():
+            return pltpu.make_async_copy(src, dst, tab_recv.at[kind, me])
+
+        return target, crosses, remote, local
+
+    for kind in range(last + 1):
+        for q in range(n):
+            target, crosses, remote, local = table_copy(kind, q)
+            if crosses:
+                remote().start()
+            else:
+                pl.when(me != target)(lambda: remote().start())
+                pl.when(me == target)(lambda: local().start())
+
     own = pltpu.make_async_copy(payoff_ref, pay.at[SUB : SUB + rows], own_sem)
     own.start()
     for copy in near:
@@ -134,69 +147,73 @@
         branch = jnp.sum(picked, axis=1, keepdims=True)
         kmask[s] = jnp.broadcast_to(branch, (ext, LANES))
 
-    state[0] = pay[pl.ds(pl.multiple_of(me * quarter, SUB), ext), :]
-    lane = lax.broadcasted_iota(jnp.int32, (ext, LANES), 1)
-
-    def waits(src):
-        for kind in range(3):
-            _, _, source, landing = piece(kind, 0)
-            dst = tab.at[pl.ds(src * per, per), landing, 0:5]
-            pltpu.make_async_copy(tables_ref.at[:, source], dst, tab_recv.at[kind, src]).wait()
+    lane = lax.broadcasted_iota(jnp.int32, (wide, LANES), 1)
+
+    def waits(kind, src):
+        _, _, source, landing = piece(kind, 0)
+        dst = tab.at[src, :, landing]
+        pltpu.make_async_copy(tables_ref.at[:, source], dst, tab_recv.at[kind, src]).wait()
 
     def shifts(x):
         f1 = pltpu.roll(x, LANES - 1, 1)
         f2 = pltpu.roll(x, LANES - 2, 1)
         b1 = pltpu.roll(x, 1, 1)
         b2 = pltpu.roll(x, 2, 1)
-        f1 = jnp.where(lane >= LANES - 1, pltpu.roll(f1, ext - 1, 0), f1)
-        f2 = jnp.where(lane >= LANES - 2, pltpu.roll(f2, ext - 1, 0), f2)
+        f1 = jnp.where(lane >= LANES - 1, pltpu.roll(f1, wide - 1, 0), f1)
+        f2 = jnp.where(lane >= LANES - 2, pltpu.roll(f2, wide - 1, 0), f2)
         b1 = jnp.where(lane < 1, pltpu.roll(b1, 1, 0), b1)
         b2 = jnp.where(lane < 2, pltpu.roll(b2, 1, 0), b2)
         return b2, b1, f1, f2
 
-    for s in reversed(range(steps)):
-        if s % per == per - 1:
-            waits(s // per)
-        w = vol_ref[s] * vol_ref[s]
-        discount = tab[s, :, 0, :]
-        slope_up = discount * tab[s, :, 2, :]
-        slope_down = discount * tab[s, :, 4, :]
-        up = discount * tab[s, :, 1, :] + w * slope_up
-        down = discount * tab[s, :, 3, :] + w * slope_down
-        middle = discount - up - down
-        branch = kmask[s]
-        low = branch < -0.5
-        high = branch > 0.5
-
-        def moved(x):
-            b2, b1, f1, f2 = shifts(x)
-            above = jnp.where(low, x, jnp.where(high, f2, f1))
-            level = jnp.where(low, b1, jnp.where(high, f1, x))
-            below = jnp.where(low, b2, jnp.where(high, x, b1))
-            return above, level, below
-
-        for g in [0] + list(range(s + 2, steps + 1)):
-            above, level, below = moved(state[g])
-            state[g] = up * above + middle * level + down * below
-            if g == 0:
-                state[s + 1] = slope_up * (above - level) + slope_down * (below - level)
-
-    here = pl.ds(pl.multiple_of(me * quarter, SUB), quarter)
-    for g in range(steps + 1):
-        rows_ref[g, here, :] = state[g, SUB : SUB + quarter, :]
-    weights = positions_ref[here, :]
-    for s in range(steps):
-        part[ring, s : s + 1, :] = jnp.sum(
-            weights * state[s + 1, SUB : SUB + quarter, :], axis=0, keepdims=True
-        )
-
-    def result(m, d, slot):
-        held = pl.ds(pl.multiple_of(jnp.bitwise_xor(me, m) * quarter, SUB), quarter)
+    def roll_back(h):
+        window = slice(h * span, h * span + wide)
+        state[0] = pay[pl.ds(pl.multiple_of(me * quarter + h * span, SUB), wide), :]
+        for s in reversed(range(steps)):
+            src, step = s // per, s % per
+            if step == per - 1:
+                if h == 0:
+                    waits(0, src)
+                waits(h + 1, src)
+                if h == chunks - 1:
+                    waits(last, src)
+            w = vol_ref[s] * vol_ref[s]
+            discount = tab[src, 0, window, step, :]
+            slope_up = discount * tab[src, 2, window, step, :]
+            slope_down = discount * tab[src, 4, window, step, :]
+            up = discount * tab[src, 1, window, step, :] + w * slope_up
+            down = discount * tab[src, 3, window, step, :] + w * slope_down
+            middle = discount - up - down
+            branch = kmask[s, window]
+            low = branch < -0.5
+            high = branch > 0.5
+            for g in [0] + list(range(s + 2, steps + 1)):
+                x = state[g]
+                b2, b1, f1, f2 = shifts(x)
+                above = jnp.where(low, x, jnp.where(high, f2, f1))
+                level = jnp.where(low, b1, jnp.where(high, f1, x))
+                below = jnp.where(low, b2, jnp.where(high, x, b1))
+                state[g] = up * above + middle * level + down * below
+                if g == 0:
+                    state[s + 1] = slope_up * (above - level) + slope_down * (below - level)
+        here = pl.ds(pl.multiple_of(me * quarter + h * span, SUB), span)
+        weights = positions_ref[here, :]
+        for g in range(steps + 1):
+            center = state[g, SUB : SUB + span, :]
+            rows_ref[g, here, :] = center
+            if g:
+                weighted = jnp.sum(weights * center, axis=0, keepdims=True)
+                if h:
+                    weighted = weighted + part[ring, g - 1 : g, :]
+                part[ring, g - 1 : g, :] = weighted
+
+    def result(m, d, slot, h):
+        first = jnp.bitwise_xor(me, m) * quarter + h * span
+        held = pl.ds(pl.multiple_of(first, SUB), span)
         return pltpu.make_async_remote_copy(
             src_ref=rows_ref.at[:, held, :],
             dst_ref=rows_ref.at[:, held, :],
-            send_sem=res_send.at[slot],
-            recv_sem=res_recv.at[slot],
+            send_sem=res_send.at[slot, h],
+            recv_sem=res_recv.at[slot, h],
             device_id=at(ring, jnp.bitwise_xor(me, d)),
             device_id_type=MESH,
         )
@@ -209,10 +226,13 @@
         masks = masks + [m | d for m in masks]
         d //= 2
     slots = {m | d: i for i, (m, d) in enumerate(plan)}
-    copies = [result(m, d, i) for i, (m, d) in enumerate(plan)]
-    for i, (m, d) in enumerate(plan):
-        if m == 0:
-            copies[i].start()
+    landed = set()
+    copies = [[result(m, d, i, h) for h in range(chunks)] for i, (m, d) in enumerate(plan)]
+    for h in range(chunks):
+        roll_back(h)
+        for i, (m, d) in enumerate(plan):
+            if m == 0:
+                copies[i][h].start()
 
     ring_copies = []
     for i in range(1, ring_size):
@@ -249,27 +269,30 @@
     for copy in grp_copies:
         copy.start()
 
-    for i, (m, d) in enumerate(plan):
-        if m != 0:
-            copies[slots[m]].wait_recv()
-            copies[i].start()
+    for h in range(chunks):
+        for i, (m, d) in enumerate(plan):
+            if m != 0:
+                if (m, h) not in landed:
+                    landed.add((m, h))
+                    copies[slots[m]][h].wait_recv()
+                copies[i][h].start()
     for i, copy in enumerate(grp_copies, 1):
         copy.wait_send()
         src = lax.rem(me + n - i, n)
         pltpu.make_async_copy(part2.at[src], part2.at[src], grp_recv.at[i]).wait()
     sums_ref[...] = jnp.sum(part2[...], axis=0)
-    forwarded = {m for m, _ in plan if m}
-    for i, (m, d) in enumerate(plan):
-        copies[i].wait_send()
-        if m | d not in forwarded:
-            copies[i].wait_recv()
-    for kind in range(3):
+    for h in range(chunks):
+        for i, (m, d) in enumerate(plan):
+            copies[i][h].wait_send()
+            if (m | d, h) not in landed:
+                copies[i][h].wait_recv()
+    for kind in range(last + 1):
         for q in range(n):
             target, crosses, remote, _ = table_copy(kind, q)
             if crosses:
-                remote.wait_send()
+                remote().wait_send()
             else:
-                pl.when(me != target)(remote.wait_send)
+                pl.when(me != target)(lambda: remote().wait_send())
 
 
 def spread_kernel(vol_ref, bucket_ref, bump_ref, rows_ref, sums_ref, out_ref, vega_ref):
@@ -301,12 +324,14 @@
     quarter = rows // n
     ext = quarter + 2 * SUB
     ring = nx * ny
-    tiles = tables.reshape(per, comps, rows, LANES).transpose(0, 2, 1, 3)
+    chunks = 2
+    wide = quarter // chunks + 2 * SUB
+    tiles = tables.transpose(1, 0, 2).reshape(comps, per, rows, LANES).transpose(0, 2, 1, 3)
     dma = pltpu.SemaphoreType.DMA
     vmem = pl.BlockSpec(memory_space=pltpu.VMEM)
     smem = pl.BlockSpec(memory_space=pltpu.SMEM)
     moved, sums = pl.pallas_call(
-        functools.partial(sweep_kernel, (n, nx, ny, steps, per, block_len)),
+        functools.partial(sweep_kernel, (n, nx, ny, steps, per, block_len, chunks)),
         out_shape=(
             jax.ShapeDtypeStruct((steps + 1, rows, LANES), jnp.float32),
             jax.ShapeDtypeStruct((steps, LANES), jnp.float32),
@@ -314,20 +339,20 @@
         in_specs=[smem, vmem, vmem, vmem, pl.BlockSpec(memory_space=pl.ANY)],
         out_specs=(vmem, vmem),
         scratch_shapes=[
-            pltpu.VMEM((steps, ext, SUB, LANES), jnp.float32),
+            pltpu.VMEM((n, comps, ext, per, LANES), jnp.float32),
             pltpu.VMEM((rows + 2 * SUB, LANES), jnp.float32),
             pltpu.VMEM((2,) + offsets.shape, jnp.int32),
             pltpu.VMEM((steps, ext, LANES), jnp.float32),
-            pltpu.VMEM((steps + 1, ext, LANES), jnp.float32),
+            pltpu.VMEM((steps + 1, wide, LANES), jnp.float32),
             pltpu.VMEM((ring, steps, LANES), jnp.float32),
             pltpu.VMEM((n, steps, LANES), jnp.float32),
-            dma((3, n)),
-            dma((3, n)),
+            dma((chunks + 2, n)),
+            dma((chunks + 2, n)),
             dma((4,)),
             dma((4,)),
             dma,
-            dma((n - 1,)),
-            dma((n - 1,)),
+            dma((n - 1, chunks)),
+            dma((n - 1, chunks)),
             dma((ring,)),
             dma((ring,)),
             dma((n,)),

time: 46 us -> 42 us (0.913)
  local copies, waits for them, and re-layouts: 4.5 us -> 0 us
  Pallas kernels: 40.6 us -> 41.1 us
    reshape x2 -> x0, local copies, waits for them, and re-layouts: 4.5 us -> none  [on_device(): tiles = tables.reshape(per, comps, rows, LANES).transpose(0, 2, 1, 3)]
    pallas_call x1, Pallas kernels: 36.3 us -> 36.8 us  [on_device(): pl.pallas_call(functools.partial(sweep_kernel, (n, nx, ny, steps, per, bl...]
where the time goes in v2:
time: 42 us; the launch traced here: 41.8 us
  Pallas kernels  41.1 us (98%)
  between operations  0.64 us (2%)
    pallas_call x1, Pallas kernels, on_device(): pl.pallas_call(functools.partial(sweep_kernel, (n, nx, ny, steps, per, bl...  36.8 us
    pallas_call x1, Pallas kernels, on_device(): pl.pallas_call(spread_kernel, grid=(grid,), out_shape=(jax.ShapeDtypeStru...  4.34 us

profile of v2, /device:TPU:0, one launch (start us, length us, event | category | flops | bytes accessed | tf_op | source)
XLA Modules:
  0.0 41.8 jit_solution(12081799128455010511)
XLA Ops:
  0.6 36.8 %sweep.1 = (f32[9,256,128]{2,1,0:T(8,128)}, f32[8,128]{1,0:T(8,128)}) custom-call(f32[8]{0:T(128)} %vol_ref.3, f32[256,128]{1,0:T(8,128)} %bitcast.12, f32[256,128]{1,0:T(8,128)} %bitcast.13, s32[8,128]{1,0:T(8,128)} %offsets_ref.1, f32[5,256,2,128]{3,2,1,0:T(2,128)} %bitcast.11), custom_call_target="tpu_custom_call" | custom-call | tf_op jit(solution)/shard_map/sweep/pallas_call | solution.py:333
  37.4 4.3 %spread.1 = (f32[2,256,8,128]{3,2,1,0:T(8,128)}, f32[1,16]{1,0:T(1,128)}) custom-call(f32[8]{0:T(128)} %vol_ref.3, s32[16]{0:T(128)} %bucket_ref.1, f32[16]{0:T(128)} %bump_ref.1, f32[9,256,128]{2,1,0:T(8,128)} %get-tuple-element.6.rows_ref, f32[8,128]{1,0:T(8,128)} %get-tuple-element.7.sums_ref), custom_call_target="tpu_custom_call" | custom-call | tf_op jit(solution)/shard_map/spread/pallas_call | solution.py:372

commit v3 on v2

--- a/solution.py
+++ b/solution.py
@@ -55,6 +55,14 @@
 
     right = lax.rem(ring + 1, ring_size)
     left = lax.rem(ring + ring_size - 1, ring_size)
+
+    barrier = pltpu.get_barrier_semaphore()
+    peers = [at(ring, lax.rem(me + i, n)) for i in range(1, n)]
+    peers += [at(lax.rem(ring + i, ring_size), me) for i in range(1, ring_size)]
+    peers += [at(r, lax.rem(me + i, n)) for i in range(1, n) for r in (left, right)]
+    for peer in peers:
+        pl.semaphore_signal(barrier, inc=1, device_id=peer, device_id_type=MESH)
+    pl.semaphore_wait(barrier, len(peers))
 
     def neighbour(i, src, dst, to):
         return pltpu.make_async_remote_copy(
@@ -203,8 +211,8 @@
             if g:
                 weighted = jnp.sum(weights * center, axis=0, keepdims=True)
                 if h:
-                    weighted = weighted + part[ring, g - 1 : g, :]
-                part[ring, g - 1 : g, :] = weighted
+                    weighted = weighted + part2[me, g - 1 : g, :]
+                part2[me, g - 1 : g, :] = weighted
 
     def result(m, d, slot, h):
         first = jnp.bitwise_xor(me, m) * quarter + h * span
@@ -228,32 +236,6 @@
     slots = {m | d: i for i, (m, d) in enumerate(plan)}
     landed = set()
     copies = [[result(m, d, i, h) for h in range(chunks)] for i, (m, d) in enumerate(plan)]
-    for h in range(chunks):
-        roll_back(h)
-        for i, (m, d) in enumerate(plan):
-            if m == 0:
-                copies[i][h].start()
-
-    ring_copies = []
-    for i in range(1, ring_size):
-        to = lax.rem(ring + i, ring_size)
-        ring_copies.append(
-            pltpu.make_async_remote_copy(
-                src_ref=part.at[ring],
-                dst_ref=part.at[ring],
-                send_sem=ring_send.at[i],
-                recv_sem=ring_recv.at[i],
-                device_id=at(to, me),
-                device_id_type=MESH,
-            )
-        )
-    for copy in ring_copies:
-        copy.start()
-    for i, copy in enumerate(ring_copies, 1):
-        copy.wait_send()
-        src = lax.rem(ring + ring_size - i, ring_size)
-        pltpu.make_async_copy(part.at[src], part.at[src], ring_recv.at[i]).wait()
-    part2[me] = jnp.sum(part[...], axis=0)
     grp_copies = []
     for i in range(1, n):
         grp_copies.append(
@@ -266,21 +248,49 @@
                 device_id_type=MESH,
             )
         )
-    for copy in grp_copies:
-        copy.start()
-
-    for h in range(chunks):
+    ring_copies = []
+    for i in range(1, ring_size):
+        ring_copies.append(
+            pltpu.make_async_remote_copy(
+                src_ref=part.at[ring],
+                dst_ref=part.at[ring],
+                send_sem=ring_send.at[i],
+                recv_sem=ring_recv.at[i],
+                device_id=at(lax.rem(ring + i, ring_size), me),
+                device_id_type=MESH,
+            )
+        )
+
+    def forward(h):
         for i, (m, d) in enumerate(plan):
             if m != 0:
                 if (m, h) not in landed:
                     landed.add((m, h))
                     copies[slots[m]][h].wait_recv()
                 copies[i][h].start()
-    for i, copy in enumerate(grp_copies, 1):
-        copy.wait_send()
+
+    for h in range(chunks):
+        roll_back(h)
+        if h == chunks - 1:
+            for copy in grp_copies:
+                copy.start()
+        for i, (m, d) in enumerate(plan):
+            if m == 0:
+                copies[i][h].start()
+    for i in range(1, n):
         src = lax.rem(me + n - i, n)
         pltpu.make_async_copy(part2.at[src], part2.at[src], grp_recv.at[i]).wait()
-    sums_ref[...] = jnp.sum(part2[...], axis=0)
+    part[ring] = jnp.sum(part2[...], axis=0)
+    for copy in ring_copies:
+        copy.start()
+    for h in range(chunks):
+        forward(h)
+    for i in range(1, ring_size):
+        src = lax.rem(ring + ring_size - i, ring_size)
+        pltpu.make_async_copy(part.at[src], part.at[src], ring_recv.at[i]).wait()
+    sums_ref[...] = jnp.sum(part[...], axis=0)
+    for copy in grp_copies + ring_copies:
+        copy.wait_send()
     for h in range(chunks):
         for i, (m, d) in enumerate(plan):
             copies[i][h].wait_send()
@@ -358,7 +368,7 @@
             dma((n,)),
             dma((n,)),
         ],
-        compiler_params=pltpu.CompilerParams(has_side_effects=True),
+        compiler_params=pltpu.CompilerParams(has_side_effects=True, collective_id=0),
         name="sweep",
     )(
         vol_curve,
@@ -367,7 +377,7 @@
         offsets,
         tiles,
     )
-    grid = n
+    grid = max(1, n // 2)
     groups = curves // SUB
     bumped, vega = pl.pallas_call(
         spread_kernel,

time: 42 us -> 37.8 us (0.90)
  Pallas kernels: 41.1 us -> 37 us
    pallas_call x1, Pallas kernels: 36.8 us -> 33.5 us  [on_device(): pl.pallas_call(functools.partial(sweep_kernel, (n, nx, ny, steps, per, bl...]
    pallas_call x1, Pallas kernels: 4.34 us -> 3.5 us  [on_device(): pl.pallas_call(spread_kernel, grid=(grid,), out_shape=(jax.ShapeDtypeStru...]
where the time goes in v3:
time: 37.8 us; the launch traced here: 37.7 us
  Pallas kernels  37 us (98%)
  between operations  0.64 us (2%)
    pallas_call x1, Pallas kernels, on_device(): pl.pallas_call(functools.partial(sweep_kernel, (n, nx, ny, steps, per, bl...  33.5 us
    pallas_call x1, Pallas kernels, on_device(): pl.pallas_call(spread_kernel, grid=(grid,), out_shape=(jax.ShapeDtypeStru...  3.5 us

profile of v3, /device:TPU:0, one launch (start us, length us, event | category | flops | bytes accessed | tf_op | source)
XLA Modules:
  0.0 37.7 jit_solution(17577216705369758722)
XLA Ops:
  0.6 33.5 %sweep.1 = (f32[9,256,128]{2,1,0:T(8,128)}, f32[8,128]{1,0:T(8,128)}) custom-call(f32[8]{0:T(128)} %vol_ref.3, f32[256,128]{1,0:T(8,128)} %bitcast.12, f32[256,128]{1,0:T(8,128)} %bitcast.13, s32[8,128]{1,0:T(8,128)} %offsets_ref.1, f32[5,256,2,128]{3,2,1,0:T(2,128)} %bitcast.11), custom_call_target="tpu_custom_call" | custom-call | tf_op jit(solution)/shard_map/sweep/pallas_call | solution.py:343
  34.2 3.5 %spread.1 = (f32[2,256,8,128]{3,2,1,0:T(8,128)}, f32[1,16]{1,0:T(1,128)}) custom-call(f32[8]{0:T(128)} %vol_ref.3, s32[16]{0:T(128)} %bucket_ref.1, f32[16]{0:T(128)} %bump_ref.1, f32[9,256,128]{2,1,0:T(8,128)} %get-tuple-element.6.rows_ref, f32[8,128]{1,0:T(8,128)} %get-tuple-element.7.sums_ref), custom_call_target="tpu_custom_call" | custom-call | tf_op jit(solution)/shard_map/spread/pallas_call | solution.py:382
